TPU v7x, 32 devices: a whole 2x2x4 slice. The times are simulated.
32 devices in a mesh: lang: 8 (over z, core), shard: 4 (over y, x).
Axes of the slice: x: 2, y: 2, z: 4, core: 2. Of those that a mesh axis runs over, the one named last changes fastest.
Arguments:
- queries: bfloat16 [4096, 768], P(('lang', 'shard')), may hold values from -6 to 6
- routes: int32 [4096, 1], P(('lang', 'shard')), may hold values from 0 to 7; in each aligned block of 128 rows (0 to 127, 128 to 255, ...) at most 20 rows name the same one
- corpus: bfloat16 [32768, 768], P(('lang', 'shard')), may hold values from -0.21875 to 0.21875
Outputs:
- top_scores: float32 [4096, 128], P(('lang', 'shard'))
Inputs may be any that keep to these rules, and one draw needn't show every extreme that they name: `routes`: among the 128 queries of one device, each language is named at most 20 times; some language is named exactly 20 times.
All inputs are finite; a program needn't handle non-finite values.
Results may differ from a plain program's by a relative error of at most 0.0012.
Values may be sent and summed in bfloat16 or wider, within the bound.
A program may use at most 64 MiB of HBM per device.

v0:
```python
import jax
import jax.numpy as jnp
from jax import lax
from jax.sharding import PartitionSpec as P

CAP = 20
TOPK = 128


epsilon = 1e-06


def score_block(query_rows, corpus, keep_count):
    leaders = None
    scores = lax.dot_general(
        query_rows, corpus, (((1,), (1,)), ((), ())), preferred_element_type=jnp.float32
    )
    leaders = lax.top_k(scores, keep_count)[0]
    return leaders


def shards(queries, routes, corpus):
    lang_count = lax.axis_size("lang")
    feature_count = queries.shape[1]
    capacity = CAP
    keep_count = TOPK
    widened = queries.astype(jnp.float32)
    unit_query = (
        widened * lax.rsqrt(jnp.mean(widened * widened, axis=1, keepdims=True) + epsilon)
    ).astype(jnp.bfloat16)
    language = routes[:, 0]
    onehot = (language[:, None] == jnp.arange(lang_count, dtype=jnp.int32)[None, :]).astype(
        jnp.int32
    )
    slot_index = jnp.sum(jnp.cumsum(onehot, axis=0) * onehot, axis=1) - 1
    position = language * capacity + slot_index
    outbox = (
        jnp.zeros((lang_count * capacity, feature_count), jnp.bfloat16).at[position].set(unit_query)
    )
    arrived = lax.all_to_all(outbox, "lang", split_axis=0, concat_axis=0, tiled=True)
    candidates = score_block(
        lax.all_gather(arrived, "shard", axis=0, tiled=True), corpus, keep_count
    )
    pooled = lax.all_to_all(candidates, "shard", split_axis=0, concat_axis=1, tiled=True)
    owned = lax.top_k(pooled, keep_count)[0]
    returned = lax.all_to_all(owned, "lang", split_axis=0, concat_axis=0, tiled=True)
    return returned[position]


def solution(mesh):
    placed = (P(("lang", "shard"), None), P(("lang", "shard"), None), P(("lang", "shard"), None))
    return jax.shard_map(
        shards, mesh=mesh, in_specs=placed, out_specs=P(("lang", "shard"), None), check_vma=False
    )
```

profile of v0, /device:TPU:0, one launch (start us, length us, event | category | flops | bytes accessed | tf_op | source)
XLA Modules:
  0.0 169.3 jit_solution(8809938689046548119)
XLA Ops:
  0.0 0.0 copy-start
  0.0 0.9 fusion.6
  0.9 0.2 reduce_window_sum.11
  1.0 0.8 select_reduce_fusion
  1.9 0.7 fusion.7
  2.5 1.0 fusion
  3.6 1.6 scatter_custom_fusion
  5.2 0.1 all_to_all.30
  5.3 16.6 %all_to_all.43 = bf16[8,20,768]{2,1,0:T(8,128)(2,1)S(1)} all-to-all(bf16[8,20,768]{2,1,0:T(8,128)(2,1)S(1)} %all_to_all.30), channel_id=1, replica_groups=mesh['lang'=8,'shard'=4] {'lang'}, dimensions={0} | all-to-all | bytes 491520 | tf_op jit(solution)/shard_map/all_to_all | solution.py:40
  21.9 0.1 all_to_all.32
  21.9 13.2 %all_gather.3 = bf16[640,768]{1,0:T(8,128)(2,1)S(1)} all-gather(bf16[160,768]{1,0:T(8,128)(2,1)S(1)} %all_to_all.32), channel_id=1, replica_groups=mesh['lang'=8,'shard'=4] {'shard'}, dimensions={0}, use_global_device_ids=true | all-gather | bytes 1228800 | tf_op jit(solution)/shard_map/all_gather | solution.py:42
  35.1 0.0 copy-done
  35.1 2.9 %fusion.8 = f32[640,1024]{0,1:T(8,128)} fusion(bf16[640,768]{1,0:T(8,128)(2,1)S(1)} %all_gather.3, bf16[1024,768]{1,0:T(8,128)(2,1)S(1)} %copy-done), kind=kOutput, calls=%fused_computation.18 | convolution fusion | flops 1006632960 | bytes 5177344
  38.0 1.7 %iota.10.clone = s32[640,1024]{0,1:T(8,128)} iota(), iota_dimension=1 | iota | bytes 2621440 | tf_op jit(solution)/shard_map/iota.4
  39.7 93.1 %top_k.14 = (f32[640,1024]{0,1:T(8,128)}, s32[640,1024]{0,1:T(8,128)}) sort(f32[640,1024]{0,1:T(8,128)} %fusion.8, s32[640,1024]{0,1:T(8,128)} %iota.10.clone), dimensions={1}, to_apply=%region_4.5 | sort | flops 13107200 | bytes 10485760 | tf_op jit(solution)/shard_map/top_k | solution.py:18
  132.9 3.3 %copy.7 = f32[640,1024]{1,0:T(8,128)} copy(f32[640,1024]{0,1:T(8,128)} %get-tuple-element.11) | data formatting | bytes 5242880 | tf_op jit(solution)/shard_map/top_k | solution.py:18
  136.1 1.0 top_k.22
  137.1 8.8 %all_to_all.44 = f32[4,160,128]{2,1,0:T(8,128)S(1)} all-to-all(f32[4,160,128]{2,1,0:T(8,128)S(1)} %bitcast.16), channel_id=1, replica_groups=mesh['lang'=8,'shard'=4] {'shard'}, dimensions={0} | all-to-all | bytes 655360 | tf_op jit(solution)/shard_map/all_to_all | solution.py:44
  146.0 11.8 %sort_prefixfusion = f32[160,128]{1,0:T(8,128)S(1)} fusion(f32[160,512]{1,0:T(8,128)S(1)} %copy_bitcast_fusion), kind=kCustom, calls=%top_k.20.sort_prefix | custom fusion | flops 1392640 | bytes 409600 | tf_op jit(solution)/shard_map/top_k | solution.py:45
  157.8 0.6 all_to_all.37
  158.4 3.4 %all-to-all-start.2 = ((f32[8,20,128]{2,1,0:T(8,128)}), f32[8,20,128]{2,1,0:T(8,128)S(1)}, u32[]{:S(2)}, u32[]{:S(2)}) async-start(f32[8,20,128]{2,1,0:T(8,128)} %all_to_all.37), calls=%async_computation.2 | async-start | bytes 196608 | tf_op jit(solution)/shard_map/all_to_all | solution.py:46
  161.8 6.2 %all-to-all-done.2 = f32[8,20,128]{2,1,0:T(8,128)S(1)} async-done(((f32[8,20,128]{2,1,0:T(8,128)}), f32[8,20,128]{2,1,0:T(8,128)S(1)}, u32[]{:S(2)}, u32[]{:S(2)}) %all-to-all-start.2) | async-done | bytes 81952 | tf_op jit(solution)/shard_map/all_to_all | solution.py:46
  168.0 1.2 gather_fusion
  (4 shorter events, 0.0 us)
Async XLA Ops:
  0.0 35.1 %copy-start = (bf16[1024,768]{1,0:T(8,128)(2,1)S(1)}, bf16[1024,768]{1,0:T(8,128)(2,1)}, u32[]{:S(2)}) copy-start(bf16[1024,768]{1,0:T(8,128)(2,1)} %param.5) | copy-start | bytes 4718596
  158.4 9.6 %all-to-all-start.2 = ((f32[8,20,128]{2,1,0:T(8,128)}), f32[8,20,128]{2,1,0:T(8,128)S(1)}, u32[]{:S(2)}, u32[]{:S(2)}) async-start(f32[8,20,128]{2,1,0:T(8,128)} %all_to_all.37), calls=%async_computation.2 | async-start | bytes 196608 | tf_op jit(solution)/shard_map/all_to_all | solution.py:46
where the time goes:
time: 170 us; the launch traced here: 169 us
  other arithmetic  110 us (65%)
  blocking collectives  38.6 us (23%)
  local copies, waits for them, and re-layouts  7.96 us (5%)
  waiting for transfers between devices  6.23 us (4%)
  starting transfers between devices  3.36 us (2%)
  matrix products  2.92 us (2%)
    top_k x1, other arithmetic, score_block(): leaders = lax.top_k(scores, keep_count)[0]  93.1 us
    all_to_all x1, blocking collectives, shards(): lax.all_to_all(outbox, 'lang', split_axis=0, concat_axis=0, tiled=True)  16.6 us
    all_gather x1, blocking collectives, shards(): lax.all_gather(arrived, 'shard', axis=0, tiled=True)  13.2 us
    top_k x1, other arithmetic, shards(): owned = lax.top_k(pooled, keep_count)[0]  11.8 us
    all_to_all x1, blocking collectives, shards(): lax.all_to_all(candidates, 'shard', split_axis=0, concat_axis=1, tiled=True)  8.81 us
    all_to_all x1, waiting for transfers between devices, shards(): lax.all_to_all(owned, 'lang', split_axis=0, concat_axis=0, tiled=True)  6.23 us
    top_k x2, local copies, waits for them, and re-layouts, score_block(): leaders = lax.top_k(scores, keep_count)[0]  4.25 us
  transfers between devices with their start and end apart: 1, of which 1 were waited for; matrix products, arithmetic and copies ran while one was open for 0% of the time, Pallas kernels for 0%

commit v1 on v0

--- a/solution.py
+++ b/solution.py
@@ -1,22 +1,125 @@
+import functools
 import jax
 import jax.numpy as jnp
 from jax import lax
+from jax.experimental import pallas as pl
+from jax.experimental.pallas import tpu as pltpu
 from jax.sharding import PartitionSpec as P
 
 CAP = 20
 TOPK = 128
+LANES = 128
+SUB = 8
+PART = 32
 
 
 epsilon = 1e-06
 
 
-def score_block(query_rows, corpus, keep_count):
-    leaders = None
-    scores = lax.dot_general(
-        query_rows, corpus, (((1,), (1,)), ((), ())), preferred_element_type=jnp.float32
-    )
-    leaders = lax.top_k(scores, keep_count)[0]
-    return leaders
+def exchange(values, i, j):
+    values[i], values[j] = jnp.maximum(values[i], values[j]), jnp.minimum(values[i], values[j])
+
+
+def sort_down(values):
+    values = list(values)
+    n = len(values)
+    p = 1
+    while p < n:
+        k = p
+        while k >= 1:
+            for j in range(k % p, n - k, 2 * k):
+                for i in range(min(k, n - j - k)):
+                    if (i + j) // (2 * p) == (i + j + k) // (2 * p):
+                        exchange(values, i + j, i + j + k)
+            k //= 2
+        p *= 2
+    return values
+
+
+def bitonic_down(values):
+    values = list(values)
+    d = len(values) // 2
+    while d:
+        for i in range(len(values)):
+            if not i & d:
+                exchange(values, i, i + d)
+        d //= 2
+    return values
+
+
+def top_block(x, y, put):
+    n = TOPK
+    for g in range(n // PART):
+        run = sort_down([x[g * PART + i] for i in range(PART)])
+        for i in range(PART):
+            x[g * PART + (i if g % 2 == 0 else PART - 1 - i)] = run[i]
+    for g in range(2):
+        base = g * 2 * PART
+        for half, take in enumerate((jnp.maximum, jnp.minimum)):
+            run = bitonic_down([take(x[base + i], x[base + PART + i]) for i in range(PART)])
+            for i in range(PART):
+                at = half * PART + i
+                y[base + (at if g == 0 else 2 * PART - 1 - at)] = run[i]
+
+    def quarters(source, target, pick):
+        for i in range(PART):
+            four = [pick(source, i + PART * j) for j in range(4)]
+            four = bitonic_down(four)
+            for j in range(4):
+                target[i + PART * j] = four[j]
+
+    def finish(source, store):
+        for g in range(4):
+            run = bitonic_down([source[g * PART + i] for i in range(PART)])
+            for i in range(PART):
+                store(g * PART + i, run[i])
+
+    def keep(target):
+        def store(i, v):
+            target[i] = v
+        return store
+
+    quarters(y, x, lambda s, i: s[i])
+    finish(x, keep(y))
+    source, target = y, x
+    for shift in (4, 2, 1):
+        quarters(
+            source, target,
+            lambda s, i: jnp.maximum(s[i], pltpu.roll(s[n - 1 - i], shift, 0)),
+        )
+        finish(target, put if shift == 1 else keep(source))
+
+
+def top_kernel(q_ref, c_ref, o_ref, x, y, t):
+    blocks = q_ref.shape[0] // LANES
+
+    def put(i, v):
+        t[pl.ds(i, 1), :] = v[i % SUB:i % SUB + 1, :]
+
+    def step(b, carry):
+        rows = pl.ds(pl.multiple_of(b * LANES, LANES), LANES)
+        scores = lax.dot_general(
+            c_ref[...], q_ref[rows, :], (((1,), (1,)), ((), ())),
+            preferred_element_type=jnp.float32,
+        )
+        x[...] = scores.reshape(x.shape)
+        top_block(x, y, put)
+        o_ref[rows, :] = t[...].T
+        return carry
+
+    lax.fori_loop(0, blocks, step, 0)
+
+
+def score_block(query_rows, corpus):
+    count = query_rows.shape[0]
+    return pl.pallas_call(
+        top_kernel,
+        out_shape=jax.ShapeDtypeStruct((count, TOPK), jnp.float32),
+        in_specs=[pl.BlockSpec(memory_space=pltpu.VMEM)] * 2,
+        out_specs=pl.BlockSpec(memory_space=pltpu.VMEM),
+        scratch_shapes=[pltpu.VMEM((TOPK, SUB, LANES), jnp.float32)] * 2
+        + [pltpu.VMEM((TOPK, LANES), jnp.float32)],
+    )(query_rows, corpus)
 
 
 def shards(queries, routes, corpus):
@@ -39,7 +142,7 @@
     )
     arrived = lax.all_to_all(outbox, "lang", split_axis=0, concat_axis=0, tiled=True)
     candidates = score_block(
-        lax.all_gather(arrived, "shard", axis=0, tiled=True), corpus, keep_count
+        lax.all_gather(arrived, "shard", axis=0, tiled=True), corpus
     )
     pooled = lax.all_to_all(candidates, "shard", split_axis=0, concat_axis=1, tiled=True)
     owned = lax.top_k(pooled, keep_count)[0]

time: 170 us -> 79.4 us (0.47)
  other arithmetic: 110 us -> 16.9 us
  Pallas kernels: 0 us -> 9.7 us
  local copies, waits for them, and re-layouts: 7.96 us -> 2.01 us
  matrix products: 2.92 us -> 0 us
  blocking collectives: 38.6 us -> 40.8 us
    top_k x1 -> x0, other arithmetic: 93.1 us -> none  [score_block(): leaders = lax.top_k(scores, keep_count)[0]]
    pallas_call x0 -> x1, Pallas kernels: none -> 9.7 us  [score_block(): pl.pallas_call(top_kernel, out_shape=jax.ShapeDtypeStruct((count, TOPK),...]
    top_k x2 -> x0, local copies, waits for them, and re-layouts: 4.25 us -> none  [score_block(): leaders = lax.top_k(scores, keep_count)[0]]
    unnamed x1 -> x0, matrix products: 2.92 us -> none
where the time goes in v1:
time: 79.4 us; the launch traced here: 79 us
  blocking collectives  40.8 us (51%)
  other arithmetic  16.9 us (21%)
  Pallas kernels  9.7 us (12%)
  waiting for transfers between devices  6.23 us (8%)
  starting transfers between devices  3.36 us (4%)
  local copies, waits for them, and re-layouts  2.01 us (3%)
    all_to_all x1, blocking collectives, shards(): lax.all_to_all(outbox, 'lang', split_axis=0, concat_axis=0, tiled=True)  16.6 us
    all_gather x1, blocking collectives, shards(): lax.all_gather(arrived, 'shard', axis=0, tiled=True)  14.5 us
    top_k x1, other arithmetic, shards(): owned = lax.top_k(pooled, keep_count)[0]  11.8 us
    pallas_call x1, Pallas kernels, score_block(): pl.pallas_call(top_kernel, out_shape=jax.ShapeDtypeStruct((count, TOPK),...  9.7 us
    all_to_all x1, blocking collectives, shards(): lax.all_to_all(candidates, 'shard', split_axis=0, concat_axis=1, tiled=True)  9.67 us
    all_to_all x1, waiting for transfers between devices, shards(): lax.all_to_all(owned, 'lang', split_axis=0, concat_axis=0, tiled=True)  6.23 us
    all_to_all x1, starting transfers between devices, shards(): lax.all_to_all(owned, 'lang', split_axis=0, concat_axis=0, tiled=True)  3.36 us
    scatter x1, other arithmetic, shards(): jnp.zeros((lang_count * capacity, feature_count), jnp.bfloat16).at[position]  1.63 us
  transfers between devices with their start and end apart: 1, of which 1 were waited for; matrix products, arithmetic and copies ran while one was open for 0% of the time, Pallas kernels for 0%

profile of v1, /device:TPU:0, one launch (start us, length us, event | category | flops | bytes accessed | tf_op | source)
XLA Modules:
  0.0 79.0 jit_solution(15604089096633933252)
XLA Ops:
  0.0 0.7 fusion.6
  0.7 0.2 reduce_window_sum.11
  0.9 0.8 %select_reduce_fusion = s32[128]{0:T(128)S(1)} fusion(s32[128,8]{1,0:T(8,128)S(1)} %reduce_window_sum.11, s32[128]{0:T(128)} %bitcast.16), kind=kLoop, calls=%fused_computation.10 | loop fusion | flops 2944 | bytes 5120 | tf_op jit(solution)/shard_map/reduce_sum | solution.py:138
  1.7 0.7 fusion.7
  2.4 1.0 %fusion = f32[128]{0:T(128)S(1)} fusion(bf16[128,768]{1,0:T(8,128)(2,1)} %param.3), kind=kLoop, calls=%fused_computation.4 | loop fusion | flops 294784 | bytes 197120 | tf_op jit(solution)/shard_map/reduce_sum | solution.py:132
  3.5 1.6 %scatter_custom_fusion = bf16[160,768]{1,0:T(8,128)(2,1)S(1)} fusion(s32[128]{0:T(128)S(1)} %fusion.7, bf16[128,768]{1,0:T(8,128)(2,1)} %param.3, f32[128]{0:T(128)S(1)} %add_rsqrt_fusion, bf16[]{:T(256)} %constant.22.clone.1), kind=kCustom, calls=%fused_computation.7 | custom fusion | flops 294912 | bytes 442882 | tf_op jit(solution)/shard_map/scatter | solution.py:141
  5.1 0.1 all_to_all.30
  5.2 16.6 %all_to_all.43 = bf16[8,20,768]{2,1,0:T(8,128)(2,1)S(1)} all-to-all(bf16[8,20,768]{2,1,0:T(8,128)(2,1)S(1)} %all_to_all.30), channel_id=1, replica_groups=mesh['lang'=8,'shard'=4] {'lang'}, dimensions={0} | all-to-all | bytes 491520 | tf_op jit(solution)/shard_map/all_to_all | solution.py:143
  21.7 0.1 all_to_all.32
  21.8 14.5 %all_gather.3.q_ref = bf16[640,768]{1,0:T(8,128)(2,1)} all-gather(bf16[160,768]{1,0:T(8,128)(2,1)S(1)} %all_to_all.32), channel_id=1, replica_groups=mesh['lang'=8,'shard'=4] {'shard'}, dimensions={0}, use_global_device_ids=true | all-gather | bytes 1228800 | tf_op jit(solution)/shard_map/all_gather | solution.py:145
  36.3 9.7 %shard_map.37 = f32[640,128]{1,0:T(8,128)} custom-call(bf16[640,768]{1,0:T(8,128)(2,1)} %all_gather.3.q_ref, bf16[1024,768]{1,0:T(8,128)(2,1)} %c_ref.1), custom_call_target="tpu_custom_call" | custom-call | tf_op jit(solution)/shard_map/pallas_call | solution.py:115
  46.0 9.7 %all_to_all.44 = f32[4,160,128]{2,1,0:T(8,128)S(1)} all-to-all(f32[4,160,128]{2,1,0:T(8,128)} %bitcast.14), channel_id=1, replica_groups=mesh['lang'=8,'shard'=4] {'shard'}, dimensions={0} | all-to-all | bytes 655360 | tf_op jit(solution)/shard_map/all_to_all | solution.py:147
  55.7 11.8 %sort_prefixfusion = f32[160,128]{1,0:T(8,128)S(1)} fusion(f32[160,512]{1,0:T(8,128)S(1)} %copy_bitcast_fusion), kind=kCustom, calls=%top_k.9.sort_prefix | custom fusion | flops 1392640 | bytes 409600 | tf_op jit(solution)/shard_map/top_k | solution.py:148
  67.5 0.6 all_to_all.37
  68.1 3.4 %all-to-all-start.2 = ((f32[8,20,128]{2,1,0:T(8,128)}), f32[8,20,128]{2,1,0:T(8,128)S(1)}, u32[]{:S(2)}, u32[]{:S(2)}) async-start(f32[8,20,128]{2,1,0:T(8,128)} %all_to_all.37), calls=%async_computation.2 | async-start | bytes 196608 | tf_op jit(solution)/shard_map/all_to_all | solution.py:149
  71.5 6.2 %all-to-all-done.2 = f32[8,20,128]{2,1,0:T(8,128)S(1)} async-done(((f32[8,20,128]{2,1,0:T(8,128)}), f32[8,20,128]{2,1,0:T(8,128)S(1)}, u32[]{:S(2)}, u32[]{:S(2)}) %all-to-all-start.2) | async-done | bytes 81952 | tf_op jit(solution)/shard_map/all_to_all | solution.py:149
  77.8 1.2 %gather_fusion = f32[128,128]{1,0:T(8,128)} fusion(f32[160,128]{1,0:T(8,128)S(1)} %all_to_all.39, s32[1024]{0:T(1024)S(1)} %pad_clamp_fusion), kind=kCustom, calls=%fused_computation | custom fusion | bytes 131584 | tf_op jit(solution)/shard_map/gather | solution.py:150
  (4 shorter events, 0.0 us)
Async XLA Ops:
  68.1 9.6 %all-to-all-start.2 = ((f32[8,20,128]{2,1,0:T(8,128)}), f32[8,20,128]{2,1,0:T(8,128)S(1)}, u32[]{:S(2)}, u32[]{:S(2)}) async-start(f32[8,20,128]{2,1,0:T(8,128)} %all_to_all.37), calls=%async_computation.2 | async-start | bytes 196608 | tf_op jit(solution)/shard_map/all_to_all | solution.py:149

commit v2 on v1

v2 whole, which is shorter than its diff:
```python
import functools
import jax
import jax.numpy as jnp
from jax import lax
from jax.experimental import pallas as pl
from jax.experimental.pallas import tpu as pltpu
from jax.sharding import PartitionSpec as P

CAP = 20
TOPK = 128
LANES = 128
SUB = 8
PART = 32
BACK = 24
SENT = 32
MESH = pl.DeviceIdType.MESH


epsilon = 1e-06


def exchange(values, i, j):
    values[i], values[j] = jnp.maximum(values[i], values[j]), jnp.minimum(values[i], values[j])


def sort_down(values):
    values = list(values)
    n = len(values)
    p = 1
    while p < n:
        k = p
        while k >= 1:
            for j in range(k % p, n - k, 2 * k):
                for i in range(min(k, n - j - k)):
                    if (i + j) // (2 * p) == (i + j + k) // (2 * p):
                        exchange(values, i + j, i + j + k)
            k //= 2
        p *= 2
    return values


def bitonic_down(values):
    values = list(values)
    d = len(values) // 2
    while d:
        for i in range(len(values)):
            if not i & d:
                exchange(values, i, i + d)
        d //= 2
    return values


def top_block(x, y, put, sign):
    n = TOPK
    for g in range(n // PART):
        run = sort_down([x[g * PART + i] for i in range(PART)])
        for i in range(PART):
            x[g * PART + (i if g % 2 == 0 else PART - 1 - i)] = run[i]
    for g in range(2):
        base = g * 2 * PART
        for half, take in enumerate((jnp.maximum, jnp.minimum)):
            run = bitonic_down([take(x[base + i], x[base + PART + i]) for i in range(PART)])
            for i in range(PART):
                at = half * PART + i
                y[base + (at if g == 0 else 2 * PART - 1 - at)] = run[i]

    def quarters(source, target, pick):
        for i in range(PART):
            four = [pick(source, i + PART * j) for j in range(4)]
            four = bitonic_down(four)
            for j in range(4):
                target[i + PART * j] = four[j]

    def finish(source, store):
        for g in range(4):
            run = bitonic_down([source[g * PART + i] for i in range(PART)])
            for i in range(PART):
                store(g * PART + i, run[i])

    def keep(target):
        def store(i, v):
            target[i] = v
        return store

    quarters(y, x, lambda s, i: s[i])
    finish(x, keep(y))
    source, target = y, x
    for shift in (4, 2, 1):
        def pick(s, i, shift=shift):
            best = jnp.maximum(s[i], pltpu.roll(s[n - 1 - i], shift, 0))
            return best * sign if shift == 1 else best

        quarters(source, target, pick)
        finish(target, put if shift == 1 else keep(source))


def merge_lanes(values, down):
    lane = lax.broadcasted_iota(jnp.int32, values.shape, 1)
    d = LANES // 2
    while d:
        above = pltpu.roll(values, LANES - d, 1)
        below = pltpu.roll(values, d, 1)
        low = (lane & d) == 0
        if down:
            values = jnp.where(low, jnp.maximum(values, above), jnp.minimum(values, below))
        else:
            values = jnp.where(low, jnp.minimum(values, above), jnp.maximum(values, below))
        d //= 2
    return values


def place(shape, slots):
    return (lax.broadcasted_iota(jnp.int32, shape, 0) == slots).astype(jnp.float32)


def kernel(
    langs, shard_count, q_ref, r_ref, c_hbm, o_ref,
    corpus, outbox, inbox, gathered, x, y, t, result, cand, merged, ret, back, unroute,
    c_sem, a_send, a_recv, b_send, b_recv, r_send, r_recv, z_send, z_recv,
):
    my_lang = lax.axis_index("lang")
    my_shard = lax.axis_index("shard")
    rows = langs * CAP
    part = LANES // shard_count
    chunks = rows // part

    load = pltpu.make_async_copy(c_hbm, corpus, c_sem)
    load.start()

    barrier = pltpu.get_barrier_semaphore()
    for step in range(1, langs):
        pl.semaphore_signal(
            barrier, inc=1, device_id=(lax.rem(my_lang + step, langs), my_shard), device_id_type=MESH
        )
    for step in range(1, shard_count):
        pl.semaphore_signal(
            barrier, inc=1, device_id=(my_lang, lax.rem(my_shard + step, shard_count)),
            device_id_type=MESH,
        )

    widened = q_ref[...].astype(jnp.float32)
    unit = (
        widened * lax.rsqrt(jnp.mean(widened * widened, axis=1, keepdims=True) + epsilon)
    ).astype(jnp.bfloat16)
    count = q_ref.shape[0]
    language = r_ref[...]
    onehot = (lax.broadcasted_iota(jnp.int32, (langs, count), 0) == language).astype(jnp.float32)
    upto = (
        lax.broadcasted_iota(jnp.int32, (count, count), 0)
        <= lax.broadcasted_iota(jnp.int32, (count, count), 1)
    ).astype(jnp.bfloat16)
    ranks = jnp.dot(onehot.astype(jnp.bfloat16), upto, preferred_element_type=jnp.float32)
    slot = jnp.sum(ranks * onehot, axis=0, keepdims=True).astype(jnp.int32) - 1
    sends = place((langs * SENT, count), language * SENT + slot).astype(jnp.bfloat16)
    outbox[...] = (
        jnp.dot(sends, unit, preferred_element_type=jnp.float32)
        .astype(jnp.bfloat16)
        .reshape(outbox.shape)
    )
    pl.semaphore_wait(barrier, langs - 1 + shard_count - 1)

    def over_lang(source, target, send_sems, recv_sems, step):
        to = lax.rem(my_lang + step, langs)
        return pltpu.make_async_remote_copy(
            src_ref=source.at[to], dst_ref=target.at[my_lang],
            send_sem=send_sems.at[to], recv_sem=recv_sems.at[my_lang],
            device_id=(to, my_shard), device_id_type=MESH,
        )

    def from_lang(source, target, send_sems, recv_sems, step):
        origin = lax.rem(my_lang + langs - step, langs)
        return pltpu.make_async_remote_copy(
            src_ref=source.at[origin], dst_ref=target.at[origin],
            send_sem=send_sems.at[origin], recv_sem=recv_sems.at[origin],
            device_id=(origin, my_shard), device_id_type=MESH,
        )

    for step in range(1, langs):
        over_lang(outbox, inbox, a_send, a_recv, step).start()
    inbox[my_lang] = outbox[my_lang]

    unroute[...] = place((langs * BACK, count), language * BACK + slot).T
    ret[...] = jnp.zeros_like(ret)
    row = lax.broadcasted_iota(jnp.int32, (rows, langs * SENT), 0)
    compact = (
        lax.broadcasted_iota(jnp.int32, (rows, langs * SENT), 1) == row // CAP * SENT + row % CAP
    ).astype(jnp.bfloat16)

    for step in range(1, langs):
        from_lang(outbox, inbox, a_send, a_recv, step).wait_recv()
    gathered[my_shard] = jnp.dot(
        compact, inbox[...].reshape(langs * SENT, -1), preferred_element_type=jnp.float32
    ).astype(jnp.bfloat16)

    def piece(c):
        return pl.ds(pl.multiple_of(c * part, part), part)

    def over_shard(c, step):
        to = lax.rem(my_shard + step, shard_count)
        return pltpu.make_async_remote_copy(
            src_ref=gathered.at[my_shard, piece(c)], dst_ref=gathered.at[my_shard, piece(c)],
            send_sem=b_send.at[to, c], recv_sem=b_recv.at[my_shard, c],
            device_id=(my_lang, to), device_id_type=MESH,
        )

    def from_shard(c, step):
        origin = lax.rem(my_shard + shard_count - step, shard_count)
        return pltpu.make_async_remote_copy(
            src_ref=gathered.at[origin, piece(c)], dst_ref=gathered.at[origin, piece(c)],
            send_sem=b_send.at[origin, c], recv_sem=b_recv.at[origin, c],
            device_id=(my_lang, origin), device_id_type=MESH,
        )

    def answer(c, step):
        to = lax.rem(my_shard + step, shard_count)
        return pltpu.make_async_remote_copy(
            src_ref=result.at[c, to], dst_ref=cand.at[my_shard, piece(c)],
            send_sem=r_send.at[to, c], recv_sem=r_recv.at[my_shard, c],
            device_id=(my_lang, to), device_id_type=MESH,
        )

    def answered(c, step):
        origin = lax.rem(my_shard + shard_count - step, shard_count)
        return pltpu.make_async_remote_copy(
            src_ref=result.at[c, origin], dst_ref=cand.at[origin, piece(c)],
            send_sem=r_send.at[origin, c], recv_sem=r_recv.at[origin, c],
            device_id=(my_lang, origin), device_id_type=MESH,
        )

    def send_pieces(c, carry):
        for step in range(1, shard_count):
            over_shard(c, step).start()
        return carry

    lax.fori_loop(0, chunks, send_pieces, 0)
    load.wait()
    sign = (1 - 2 * lax.rem(my_shard, 2)).astype(jnp.float32)

    def put(i, v):
        t[pl.ds(i, 1), :] = v[i % SUB:i % SUB + 1, :]

    def score(c, carry):
        for step in range(1, shard_count):
            from_shard(c, step).wait_recv()
        block = jnp.concatenate([gathered[s, piece(c)] for s in range(shard_count)], axis=0)
        scores = lax.dot_general(
            corpus[...], block, (((1,), (1,)), ((), ())), preferred_element_type=jnp.float32
        )
        x[...] = scores.reshape(x.shape)
        top_block(x, y, put, sign)
        result[c] = (t[...] * sign).T.reshape(shard_count, part, TOPK)
        for step in range(1, shard_count):
            answer(c, step).start()
        cand[my_shard, piece(c)] = result[c, my_shard]
        return carry

    lax.fori_loop(0, chunks, score, 0)

    def settle(c, carry):
        for step in range(1, shard_count):
            answered(c, step).wait_recv()
        return carry

    lax.fori_loop(0, chunks, settle, 0)
    lists = [cand[s] for s in range(shard_count)]
    while len(lists) > 1:
        lists = [
            merge_lanes(jnp.maximum(lists[2 * k], lists[2 * k + 1]), k % 2 == 0)
            for k in range(len(lists) // 2)
        ]
    merged[...] = lists[0]
    for l in range(langs):
        ret[l, 0:CAP, :] = merged[l * CAP:(l + 1) * CAP, :]
    for step in range(1, langs):
        over_lang(ret, back, z_send, z_recv, step).start()
    back[my_lang] = ret[my_lang]

    def drain(c, carry):
        for step in range(1, shard_count):
            over_shard(c, step).wait_send()
            answer(c, step).wait_send()
        return carry

    lax.fori_loop(0, chunks, drain, 0)
    for step in range(1, langs):
        over_lang(outbox, inbox, a_send, a_recv, step).wait_send()
    for step in range(1, langs):
        from_lang(ret, back, z_send, z_recv, step).wait_recv()
    o_ref[...] = jnp.dot(
        unroute[...], back[...].reshape(langs * BACK, TOPK),
        preferred_element_type=jnp.float32, precision=lax.Precision.HIGHEST,
    )
    for step in range(1, langs):
        over_lang(ret, back, z_send, z_recv, step).wait_send()


def shards(queries, routes, corpus):
    langs = lax.axis_size("lang")
    shard_count = lax.axis_size("shard")
    count, features = queries.shape
    rows = langs * CAP
    part = LANES // shard_count
    chunks = rows // part
    dma = pltpu.SemaphoreType.DMA
    per_piece = [dma((shard_count, chunks))] * 4
    f32, bf16 = jnp.float32, jnp.bfloat16
    return pl.pallas_call(
        functools.partial(kernel, langs, shard_count),
        out_shape=jax.ShapeDtypeStruct((count, TOPK), f32),
        in_specs=[
            pl.BlockSpec(memory_space=pltpu.VMEM),
            pl.BlockSpec(memory_space=pltpu.VMEM),
            pl.BlockSpec(memory_space=pl.ANY),
        ],
        out_specs=pl.BlockSpec(memory_space=pltpu.VMEM),
        scratch_shapes=[
            pltpu.VMEM(corpus.shape, bf16),
            pltpu.VMEM((langs, SENT, features), bf16),
            pltpu.VMEM((langs, SENT, features), bf16),
            pltpu.VMEM((shard_count, rows, features), bf16),
            pltpu.VMEM((TOPK, SUB, LANES), f32),
            pltpu.VMEM((TOPK, SUB, LANES), f32),
            pltpu.VMEM((TOPK, LANES), f32),
            pltpu.VMEM((chunks, shard_count, part, TOPK), f32),
            pltpu.VMEM((shard_count, rows, TOPK), f32),
            pltpu.VMEM((rows, TOPK), f32),
            pltpu.VMEM((langs, BACK, TOPK), f32),
            pltpu.VMEM((langs, BACK, TOPK), f32),
            pltpu.VMEM((count, langs * BACK), f32),
            dma, dma((langs,)), dma((langs,)), *per_piece, dma((langs,)), dma((langs,)),
        ],
        compiler_params=pltpu.CompilerParams(collective_id=0, has_side_effects=True),
    )(queries, routes.reshape(1, count), corpus)


def solution(mesh):
    placed = (P(("lang", "shard"), None), P(("lang", "shard"), None), P(("lang", "shard"), None))
    return jax.shard_map(
        shards, mesh=mesh, in_specs=placed, out_specs=P(("lang", "shard"), None), check_vma=False
    )
```

time: 79.4 us -> 43.5 us (0.55)
  blocking collectives: 40.8 us -> 0 us
  Pallas kernels: 9.7 us -> 41.8 us
  other arithmetic: 16.9 us -> 0 us
  waiting for transfers between devices: 6.23 us -> 0 us
  starting transfers between devices: 3.36 us -> 0 us
    pallas_call x1, Pallas kernels: 9.7 us -> 41.8 us  [shards(): pl.pallas_call(functools.partial(kernel, langs, shard_count), out_shape=j...]
    all_to_all x2 -> x0, blocking collectives: 26.2 us -> none  [the longest x1 16.6 us: shards(): lax.all_to_all(outbox, 'lang', split_axis=0, concat_axis=0, tiled=True)]
    all_gather x1 -> x0, blocking collectives: 14.5 us -> none  [shards(): lax.all_gather(arrived, 'shard', axis=0, tiled=True)]
    top_k x1 -> x0, other arithmetic: 11.8 us -> none  [shards(): owned = lax.top_k(pooled, keep_count)[0]]
    all_to_all x1 -> x0, waiting for transfers between devices: 6.23 us -> none  [shards(): lax.all_to_all(owned, 'lang', split_axis=0, concat_axis=0, tiled=True)]
    all_to_all x1 -> x0, starting transfers between devices: 3.36 us -> none  [shards(): lax.all_to_all(owned, 'lang', split_axis=0, concat_axis=0, tiled=True)]
    reduce_sum x2 -> x0, other arithmetic: 1.87 us -> none  [the longest x1 1.05 us: shards(): jnp.mean(widened * widened, axis=1, keepdims=True) + epsilon]
    scatter x1 -> x0, other arithmetic: 1.63 us -> none  [shards(): jnp.zeros((lang_count * capacity, feature_count), jnp.bfloat16).at[position]]
  transfers between devices with their start and end apart: 1 -> 0, of which waited for: 1 -> 0; matrix products, arithmetic and copies ran while one was open for 0% -> 0% of each run, Pallas kernels for 0% -> 0%
where the time goes in v2:
time: 43.5 us; the launch traced here: 43.3 us
  Pallas kernels  41.8 us (96%)
  local copies, waits for them, and re-layouts  1.47 us (3%)
    pallas_call x1, Pallas kernels, shards(): pl.pallas_call(functools.partial(kernel, langs, shard_count), out_shape=j...  41.8 us
    unnamed x1, local copies, waits for them, and re-layouts  1.47 us

profile of v2, /device:TPU:0, one launch (start us, length us, event | category | flops | bytes accessed | tf_op | source)
XLA Modules:
  0.0 43.3 jit_solution(11279614544633234408)
XLA Ops:
  0.0 41.8 %shard_map.37 = f32[128,128]{1,0:T(8,128)} custom-call(bf16[128,768]{1,0:T(8,128)(2,1)} %q_ref.1, s32[1,128]{1,0:T(1,128)} %bitcast.1, bf16[1024,768]{1,0:T(8,128)(2,1)} %c_hbm.1), custom_call_target="tpu_custom_call" | custom-call | tf_op jit(solution)/shard_map/pallas_call | solution.py:307
  41.8 1.5 %copy.5 = f32[128,128]{1,0:T(8,128)} copy(f32[128,128]{1,0:T(8,128)} %shard_map.37) | data formatting | bytes 131072

commit v3 on v2

v3 whole, which is shorter than its diff:
```python
import functools
import jax
import jax.numpy as jnp
from jax import lax
from jax.experimental import pallas as pl
from jax.experimental.pallas import tpu as pltpu
from jax.sharding import PartitionSpec as P

CAP = 20
TOPK = 128
LANES = 128
SUB = 8
PART = 32
MAIN = 16
REST = CAP - MAIN
PACK = 32
TAIL = 8
MESH = pl.DeviceIdType.MESH


epsilon = 1e-06


def exchange(values, i, j):
    values[i], values[j] = jnp.maximum(values[i], values[j]), jnp.minimum(values[i], values[j])


def sort_down(values):
    values = list(values)
    n = len(values)
    p = 1
    while p < n:
        k = p
        while k >= 1:
            for j in range(k % p, n - k, 2 * k):
                for i in range(min(k, n - j - k)):
                    if (i + j) // (2 * p) == (i + j + k) // (2 * p):
                        exchange(values, i + j, i + j + k)
            k //= 2
        p *= 2
    return values


def bitonic_down(values):
    values = list(values)
    d = len(values) // 2
    while d:
        for i in range(len(values)):
            if not i & d:
                exchange(values, i, i + d)
        d //= 2
    return values


def top_block(x, y, put, sign):
    n = TOPK
    for g in range(n // PART):
        run = sort_down([x[g * PART + i] for i in range(PART)])
        for i in range(PART):
            x[g * PART + (i if g % 2 == 0 else PART - 1 - i)] = run[i]
    for g in range(2):
        base = g * 2 * PART
        for half, take in enumerate((jnp.maximum, jnp.minimum)):
            run = bitonic_down([take(x[base + i], x[base + PART + i]) for i in range(PART)])
            for i in range(PART):
                at = half * PART + i
                y[base + (at if g == 0 else 2 * PART - 1 - at)] = run[i]

    def quarters(source, target, pick):
        for i in range(PART):
            four = [pick(source, i + PART * j) for j in range(4)]
            four = bitonic_down(four)
            for j in range(4):
                target[i + PART * j] = four[j]

    def finish(source, store):
        for g in range(4):
            run = bitonic_down([source[g * PART + i] for i in range(PART)])
            for i in range(PART):
                store(g * PART + i, run[i])

    def keep(target):
        def store(i, v):
            target[i] = v
        return store

    quarters(y, x, lambda s, i: s[i])
    finish(x, keep(y))
    source, target = y, x
    for shift in (4, 2, 1):
        def pick(s, i, shift=shift):
            best = jnp.maximum(s[i], pltpu.roll(s[n - 1 - i], shift, 0))
            return best * sign if shift == 1 else best

        quarters(source, target, pick)
        finish(target, put if shift == 1 else keep(source))


def merge_lanes(values, down):
    lane = lax.broadcasted_iota(jnp.int32, values.shape, 1)
    d = LANES // 2
    while d:
        above = pltpu.roll(values, LANES - d, 1)
        below = pltpu.roll(values, d, 1)
        low = (lane & d) == 0
        if down:
            values = jnp.where(low, jnp.maximum(values, above), jnp.minimum(values, below))
        else:
            values = jnp.where(low, jnp.minimum(values, above), jnp.maximum(values, below))
        d //= 2
    return values


def place(shape, slots):
    return (lax.broadcasted_iota(jnp.int32, shape, 0) == slots).astype(jnp.float32)


def kernel(
    langs, shard_count, q_ref, r_ref, c_hbm, o_ref,
    corpus, out_main, out_rest, all_main, all_rest, block, x, y, t, result, cand,
    ret_main, ret_rest, back_main, back_rest, un_main, un_rest,
    c_sem, am_send, am_recv, ar_send, ar_recv, bm_send, bm_recv, br_send, br_recv,
    r_send, r_recv, zm_send, zm_recv, zr_send, zr_recv,
):
    my_lang = lax.axis_index("lang")
    my_shard = lax.axis_index("shard")
    group = LANES // MAIN // shard_count
    groups = langs // group
    tails = langs * REST * shard_count // LANES
    tail_langs = langs // tails
    part = LANES // shard_count
    chunks = groups + tails
    my_group, my_place = my_lang // group, lax.rem(my_lang, group)
    steps = [(d, k) for d in range(groups) for k in range(group) if d or k]

    load = pltpu.make_async_copy(c_hbm, corpus, c_sem)
    load.start()

    def later(d, k):
        return lax.rem(my_group + d, groups) * group + lax.rem(my_place + k, group)

    def earlier(d, k):
        return lax.rem(my_group + groups - d, groups) * group + lax.rem(my_place + group - k, group)

    def next_shard(step):
        return lax.rem(my_shard + step, shard_count)

    def last_shard(step):
        return lax.rem(my_shard + shard_count - step, shard_count)

    barrier = pltpu.get_barrier_semaphore()
    for d, k in steps:
        pl.semaphore_signal(barrier, inc=1, device_id=(later(d, k), my_shard), device_id_type=MESH)
    for step in range(1, shard_count):
        pl.semaphore_signal(
            barrier, inc=1, device_id=(my_lang, next_shard(step)), device_id_type=MESH
        )

    widened = q_ref[...].astype(jnp.float32)
    unit = (
        widened * lax.rsqrt(jnp.mean(widened * widened, axis=1, keepdims=True) + epsilon)
    ).astype(jnp.bfloat16)
    count, features = q_ref.shape
    language = r_ref[...]
    onehot = (lax.broadcasted_iota(jnp.int32, (langs, count), 0) == language).astype(jnp.float32)
    upto = (
        lax.broadcasted_iota(jnp.int32, (count, count), 0)
        <= lax.broadcasted_iota(jnp.int32, (count, count), 1)
    ).astype(jnp.bfloat16)
    ranks = jnp.dot(onehot.astype(jnp.bfloat16), upto, preferred_element_type=jnp.float32)
    slot = jnp.sum(ranks * onehot, axis=0, keepdims=True).astype(jnp.int32) - 1
    first = slot < MAIN
    main_row = jnp.where(first, language * MAIN + slot, -1)
    out_main[...] = (
        jnp.dot(
            place((langs * MAIN, count), main_row).astype(jnp.bfloat16), unit,
            preferred_element_type=jnp.float32,
        ).astype(jnp.bfloat16).reshape(out_main.shape)
    )
    packed = jnp.zeros((langs * PACK, LANES), jnp.float32)
    for c in range(features // LANES):
        rest_row = jnp.where(first, -1, language * PACK + c * REST + slot - MAIN)
        packed += jnp.dot(
            place((langs * PACK, count), rest_row).astype(jnp.bfloat16),
            unit[:, c * LANES:(c + 1) * LANES], preferred_element_type=jnp.float32,
        )
    out_rest[...] = packed.astype(jnp.bfloat16).reshape(out_rest.shape)
    pl.semaphore_wait(barrier, langs - 1 + shard_count - 1)

    def over_lang(source, target, send_sems, recv_sems, d, k):
        to = later(d, k)
        return pltpu.make_async_remote_copy(
            src_ref=source.at[to], dst_ref=target.at[my_lang],
            send_sem=send_sems.at[to], recv_sem=recv_sems.at[my_lang],
            device_id=(to, my_shard), device_id_type=MESH,
        )

    def from_lang(source, target, send_sems, recv_sems, d, k):
        origin = earlier(d, k)
        return pltpu.make_async_remote_copy(
            src_ref=source.at[origin], dst_ref=target.at[origin],
            send_sem=send_sems.at[origin], recv_sem=recv_sems.at[origin],
            device_id=(origin, my_shard), device_id_type=MESH,
        )

    a_main = (out_main, all_main.at[my_shard], am_send, am_recv)
    a_rest = (out_rest, all_rest.at[my_shard], ar_send, ar_recv)
    z_main = (ret_main, back_main, zm_send, zm_recv)
    z_rest = (ret_rest, back_rest, zr_send, zr_recv)
    b_main = (all_main, bm_send, bm_recv)
    b_rest = (all_rest, br_send, br_recv)

    def over_shard(source, every, send_sems, recv_sems, lang, step):
        to = next_shard(step)
        return pltpu.make_async_remote_copy(
            src_ref=source, dst_ref=every.at[my_shard, lang],
            send_sem=send_sems.at[to, lang], recv_sem=recv_sems.at[my_shard, lang],
            device_id=(my_lang, to), device_id_type=MESH,
        )

    def from_shard(every, send_sems, recv_sems, lang, step):
        origin = last_shard(step)
        return pltpu.make_async_remote_copy(
            src_ref=every.at[origin, lang], dst_ref=every.at[origin, lang],
            send_sem=send_sems.at[origin, lang], recv_sem=recv_sems.at[origin, lang],
            device_id=(my_lang, origin), device_id_type=MESH,
        )

    for step in range(1, shard_count):
        over_shard(out_main.at[my_lang], *b_main, my_lang, step).start()
    for d, k in steps:
        over_lang(*a_main, d, k).start()
        over_lang(*a_rest, d, k).start()
    for step in range(1, shard_count):
        over_shard(out_rest.at[my_lang], *b_rest, my_lang, step).start()
    all_main[my_shard, my_lang] = out_main[my_lang]
    all_rest[my_shard, my_lang] = out_rest[my_lang]

    def forward(d, k):
        lang = earlier(d, k)
        from_lang(*a_main, d, k).wait_recv()
        for step in range(1, shard_count):
            over_shard(all_main.at[my_shard, lang], *b_main, lang, step).start()
        from_lang(*a_rest, d, k).wait_recv()
        for step in range(1, shard_count):
            over_shard(all_rest.at[my_shard, lang], *b_rest, lang, step).start()

    def forward_group(d):
        for k in range(group):
            forward(d, k)

    for k in range(1, group):
        forward(0, k)

    un_main[...] = place((langs * MAIN, count), main_row).T
    un_rest[...] = place(
        (langs * TAIL, count), jnp.where(first, -1, language * TAIL + slot - MAIN)
    ).T
    ret_rest[...] = jnp.zeros_like(ret_rest)

    ahead = min(2, groups - 1)
    for d in range(1, ahead + 1):
        forward_group(d)
    load.wait()
    sign = (1 - 2 * lax.rem(my_shard, 2)).astype(jnp.float32)

    def answer(c, step):
        to = next_shard(step)
        return pltpu.make_async_remote_copy(
            src_ref=result.at[c, to], dst_ref=cand.at[my_shard, c],
            send_sem=r_send.at[to, c], recv_sem=r_recv.at[my_shard, c],
            device_id=(my_lang, to), device_id_type=MESH,
        )

    def answered(c, step):
        origin = last_shard(step)
        return pltpu.make_async_remote_copy(
            src_ref=result.at[c, origin], dst_ref=cand.at[origin, c],
            send_sem=r_send.at[origin, c], recv_sem=r_recv.at[origin, c],
            device_id=(my_lang, origin), device_id_type=MESH,
        )

    def put(i, v):
        t[pl.ds(i, 1), :] = v[i % SUB:i % SUB + 1, :]

    def score(c, carry):
        @pl.when(c < groups)
        def _():
            base = lax.rem(my_group + groups - c, groups) * group
            for k in range(group):
                for step in range(1, shard_count):
                    from_shard(*b_main, base + k, step).wait_recv()
            for s in range(shard_count):
                block[s * part:(s + 1) * part, :] = all_main[s, pl.ds(base, group)].reshape(
                    part, features
                )

        @pl.when(c == groups)
        def _():
            for lang in range(langs):
                for step in range(1, shard_count):
                    from_shard(*b_rest, lang, step).wait_recv()

        @pl.when(c >= groups)
        def _():
            begin = (c - groups) * tail_langs
            shape = (LANES, shard_count * tail_langs * PACK)
            row = lax.broadcasted_iota(jnp.int32, shape, 0)
            column = lax.broadcasted_iota(jnp.int32, shape, 1)
            pieces = all_rest[:, pl.ds(begin, tail_langs)].reshape(shape[1], LANES)
            for f in range(features // LANES):
                pick = (column == row // REST * PACK + f * REST + row % REST).astype(jnp.bfloat16)
                block[:, f * LANES:(f + 1) * LANES] = jnp.dot(
                    pick, pieces, preferred_element_type=jnp.float32
                ).astype(jnp.bfloat16)

        scores = lax.dot_general(
            corpus[...], block[...], (((1,), (1,)), ((), ())), preferred_element_type=jnp.float32
        )
        x[...] = scores.reshape(x.shape)
        top_block(x, y, put, sign)
        result[c] = (t[...] * sign).T.reshape(shard_count, part, TOPK)
        for step in range(1, shard_count):
            answer(c, step).start()
        cand[my_shard, c] = result[c, my_shard]

        @pl.when(c + ahead + 1 < groups)
        def _():
            forward_group(c + ahead + 1)

        return carry

    lax.fori_loop(0, chunks, score, 0)

    def settle(c, carry):
        for step in range(1, shard_count):
            answered(c, step).wait_recv()
        return carry

    def merge(begin, end):
        lists = [
            cand[s, begin:end].reshape((end - begin) * part, TOPK) for s in range(shard_count)
        ]
        while len(lists) > 1:
            lists = [
                merge_lanes(jnp.maximum(lists[2 * j], lists[2 * j + 1]), j % 2 == 0)
                for j in range(len(lists) // 2)
            ]
        return lists[0]

    lax.fori_loop(0, groups, settle, 0)
    merged = merge(0, groups)
    for d in range(groups):
        base = lax.rem(my_group + groups - d, groups) * group
        ret_main[pl.ds(base, group)] = merged[d * part:(d + 1) * part].reshape(group, MAIN, TOPK)
    for d, k in steps:
        over_lang(*z_main, d, k).start()
    lax.fori_loop(groups, chunks, settle, 0)
    merged = merge(groups, chunks)
    for lang in range(langs):
        ret_rest[lang, 0:REST, :] = merged[lang * REST:(lang + 1) * REST, :]
    for d, k in steps:
        over_lang(*z_rest, d, k).start()
    back_main[my_lang] = ret_main[my_lang]
    back_rest[my_lang] = ret_rest[my_lang]

    def drain(lang, carry):
        for step in range(1, shard_count):
            over_shard(all_main.at[my_shard, lang], *b_main, lang, step).wait_send()
            over_shard(all_rest.at[my_shard, lang], *b_rest, lang, step).wait_send()
        return carry

    def drain_answers(c, carry):
        for step in range(1, shard_count):
            answer(c, step).wait_send()
        return carry

    lax.fori_loop(0, langs, drain, 0)
    lax.fori_loop(0, chunks, drain_answers, 0)
    for d, k in steps:
        over_lang(*a_main, d, k).wait_send()
        over_lang(*a_rest, d, k).wait_send()
    for d, k in steps:
        from_lang(*z_main, d, k).wait_recv()
    upper = jnp.dot(
        un_main[...], back_main[...].reshape(langs * MAIN, TOPK),
        preferred_element_type=jnp.float32, precision=lax.Precision.HIGHEST,
    )
    for d, k in steps:
        from_lang(*z_rest, d, k).wait_recv()
    o_ref[...] = upper + jnp.dot(
        un_rest[...], back_rest[...].reshape(langs * TAIL, TOPK),
        preferred_element_type=jnp.float32, precision=lax.Precision.HIGHEST,
    )
    for d, k in steps:
        over_lang(*z_main, d, k).wait_send()
        over_lang(*z_rest, d, k).wait_send()


def shards(queries, routes, corpus):
    langs = lax.axis_size("lang")
    shard_count = lax.axis_size("shard")
    count, features = queries.shape
    part = LANES // shard_count
    chunks = langs * CAP // part
    dma = pltpu.SemaphoreType.DMA
    f32, bf16 = jnp.float32, jnp.bfloat16
    return pl.pallas_call(
        functools.partial(kernel, langs, shard_count),
        out_shape=jax.ShapeDtypeStruct((count, TOPK), f32),
        in_specs=[
            pl.BlockSpec(memory_space=pltpu.VMEM),
            pl.BlockSpec(memory_space=pltpu.VMEM),
            pl.BlockSpec(memory_space=pl.ANY),
        ],
        out_specs=pl.BlockSpec(memory_space=pltpu.VMEM),
        scratch_shapes=[
            pltpu.VMEM(corpus.shape, bf16),
            pltpu.VMEM((langs, MAIN, features), bf16),
            pltpu.VMEM((langs, PACK, LANES), bf16),
            pltpu.VMEM((shard_count, langs, MAIN, features), bf16),
            pltpu.VMEM((shard_count, langs, PACK, LANES), bf16),
            pltpu.VMEM((LANES, features), bf16),
            pltpu.VMEM((TOPK, SUB, LANES), f32),
            pltpu.VMEM((TOPK, SUB, LANES), f32),
            pltpu.VMEM((TOPK, LANES), f32),
            pltpu.VMEM((chunks, shard_count, part, TOPK), f32),
            pltpu.VMEM((shard_count, chunks, part, TOPK), f32),
            pltpu.VMEM((langs, MAIN, TOPK), f32),
            pltpu.VMEM((langs, TAIL, TOPK), f32),
            pltpu.VMEM((langs, MAIN, TOPK), f32),
            pltpu.VMEM((langs, TAIL, TOPK), f32),
            pltpu.VMEM((count, langs * MAIN), f32),
            pltpu.VMEM((count, langs * TAIL), f32),
            dma, *[dma((langs,))] * 4, *[dma((shard_count, langs))] * 4,
            *[dma((shard_count, chunks))] * 2, *[dma((langs,))] * 4,
        ],
        compiler_params=pltpu.CompilerParams(collective_id=0, has_side_effects=True),
    )(queries, routes.reshape(1, count), corpus)


def solution(mesh):
    placed = (P(("lang", "shard"), None), P(("lang", "shard"), None), P(("lang", "shard"), None))
    return jax.shard_map(
        shards, mesh=mesh, in_specs=placed, out_specs=P(("lang", "shard"), None), check_vma=False
    )
```

time: 43.5 us -> 37.1 us (0.85)
  Pallas kernels: 41.8 us -> 35.5 us
    pallas_call x1, Pallas kernels: 41.8 us -> 35.5 us  [shards(): pl.pallas_call(functools.partial(kernel, langs, shard_count), out_shape=j...]
where the time goes in v3:
time: 37.1 us; the launch traced here: 37 us
  Pallas kernels  35.5 us (96%)
  local copies, waits for them, and re-layouts  1.47 us (4%)
    pallas_call x1, Pallas kernels, shards(): pl.pallas_call(functools.partial(kernel, langs, shard_count), out_shape=j...  35.5 us
    unnamed x1, local copies, waits for them, and re-layouts  1.47 us

profile of v3, /device:TPU:0, one launch (start us, length us, event | category | flops | bytes accessed | tf_op | source)
XLA Modules:
  0.0 37.0 jit_solution(231141823421763605)
XLA Ops:
  0.0 35.5 %shard_map.37 = f32[128,128]{1,0:T(8,128)} custom-call(bf16[128,768]{1,0:T(8,128)(2,1)} %q_ref.1, s32[1,128]{1,0:T(1,128)} %bitcast.1, bf16[1024,768]{1,0:T(8,128)(2,1)} %c_hbm.1), custom_call_target="tpu_custom_call" | custom-call | tf_op jit(solution)/shard_map/pallas_call | solution.py:408
  35.5 1.5 %copy.5 = f32[128,128]{1,0:T(8,128)} copy(f32[128,128]{1,0:T(8,128)} %shard_map.37) | data formatting | bytes 131072

commit v4 on v3

--- a/solution.py
+++ b/solution.py
@@ -141,6 +141,12 @@
 
     def earlier(d, k):
         return lax.rem(my_group + groups - d, groups) * group + lax.rem(my_place + group - k, group)
+
+    square = shard_count == 4
+    hops = (1, 2) if square else range(1, shard_count)
+
+    def across(step):
+        return my_shard + step - 2 * step * lax.rem(my_shard // step, 2)
 
     def next_shard(step):
         return lax.rem(my_shard + step, shard_count)
@@ -177,6 +183,74 @@
             preferred_element_type=jnp.float32,
         ).astype(jnp.bfloat16).reshape(out_main.shape)
     )
+    pl.semaphore_wait(barrier, langs - 1 + shard_count - 1)
+
+    def over_lang(source, target, send_sems, recv_sems, d, k):
+        to = later(d, k)
+        return pltpu.make_async_remote_copy(
+            src_ref=source.at[to], dst_ref=target.at[my_lang],
+            send_sem=send_sems.at[to], recv_sem=recv_sems.at[my_lang],
+            device_id=(to, my_shard), device_id_type=MESH,
+        )
+
+    def from_lang(source, target, send_sems, recv_sems, d, k):
+        origin = earlier(d, k)
+        return pltpu.make_async_remote_copy(
+            src_ref=source.at[origin], dst_ref=target.at[origin],
+            send_sem=send_sems.at[origin], recv_sem=recv_sems.at[origin],
+            device_id=(origin, my_shard), device_id_type=MESH,
+        )
+
+    a_main = (out_main, all_main.at[my_shard], am_send, am_recv)
+    a_rest = (out_rest, all_rest.at[my_shard], ar_send, ar_recv)
+    z_main = (ret_main, back_main, zm_send, zm_recv)
+    z_rest = (ret_rest, back_rest, zr_send, zr_recv)
+    b_main = (all_main, bm_send, bm_recv)
+    b_rest = (all_rest, br_send, br_recv)
+
+    def over_shard(source, every, send_sems, recv_sems, lang, step):
+        to = across(step) if square else next_shard(step)
+        return pltpu.make_async_remote_copy(
+            src_ref=source, dst_ref=every.at[my_shard, lang],
+            send_sem=send_sems.at[to, lang], recv_sem=recv_sems.at[my_shard, lang],
+            device_id=(my_lang, to), device_id_type=MESH,
+        )
+
+    def relay(every, send_sems, recv_sems, lang):
+        turn = 1 + lax.rem(lang, 2)
+        origin, to = across(turn), across(3 - turn)
+        return pltpu.make_async_remote_copy(
+            src_ref=every.at[origin, lang], dst_ref=every.at[origin, lang],
+            send_sem=send_sems.at[my_shard, lang], recv_sem=recv_sems.at[origin, lang],
+            device_id=(my_lang, to), device_id_type=MESH,
+        )
+
+    def relay_group(d):
+        for k in range(group):
+            lang = earlier(d, k)
+            for b in (b_main, b_rest):
+                from_origin(*b, lang, across(1 + lax.rem(lang, 2))).wait_recv()
+                relay(*b, lang).start()
+
+    def await_others(b, lang):
+        if square:
+            from_origin(*b, lang, across(2 - lax.rem(lang, 2))).wait_recv()
+            from_origin(*b, lang, 3 - my_shard).wait_recv()
+        else:
+            for step in range(1, shard_count):
+                from_origin(*b, lang, last_shard(step)).wait_recv()
+
+    def from_origin(every, send_sems, recv_sems, lang, origin):
+        return pltpu.make_async_remote_copy(
+            src_ref=every.at[origin, lang], dst_ref=every.at[origin, lang],
+            send_sem=send_sems.at[origin, lang], recv_sem=recv_sems.at[origin, lang],
+            device_id=(my_lang, origin), device_id_type=MESH,
+        )
+
+    for step in hops:
+        over_shard(out_main.at[my_lang], *b_main, my_lang, step).start()
+    for d, k in steps:
+        over_lang(*a_main, d, k).start()
     packed = jnp.zeros((langs * PACK, LANES), jnp.float32)
     for c in range(features // LANES):
         rest_row = jnp.where(first, -1, language * PACK + c * REST + slot - MAIN)
@@ -185,53 +259,9 @@
             unit[:, c * LANES:(c + 1) * LANES], preferred_element_type=jnp.float32,
         )
     out_rest[...] = packed.astype(jnp.bfloat16).reshape(out_rest.shape)
-    pl.semaphore_wait(barrier, langs - 1 + shard_count - 1)
-
-    def over_lang(source, target, send_sems, recv_sems, d, k):
-        to = later(d, k)
-        return pltpu.make_async_remote_copy(
-            src_ref=source.at[to], dst_ref=target.at[my_lang],
-            send_sem=send_sems.at[to], recv_sem=recv_sems.at[my_lang],
-            device_id=(to, my_shard), device_id_type=MESH,
-        )
-
-    def from_lang(source, target, send_sems, recv_sems, d, k):
-        origin = earlier(d, k)
-        return pltpu.make_async_remote_copy(
-            src_ref=source.at[origin], dst_ref=target.at[origin],
-            send_sem=send_sems.at[origin], recv_sem=recv_sems.at[origin],
-            device_id=(origin, my_shard), device_id_type=MESH,
-        )
-
-    a_main = (out_main, all_main.at[my_shard], am_send, am_recv)
-    a_rest = (out_rest, all_rest.at[my_shard], ar_send, ar_recv)
-    z_main = (ret_main, back_main, zm_send, zm_recv)
-    z_rest = (ret_rest, back_rest, zr_send, zr_recv)
-    b_main = (all_main, bm_send, bm_recv)
-    b_rest = (all_rest, br_send, br_recv)
-
-    def over_shard(source, every, send_sems, recv_sems, lang, step):
-        to = next_shard(step)
-        return pltpu.make_async_remote_copy(
-            src_ref=source, dst_ref=every.at[my_shard, lang],
-            send_sem=send_sems.at[to, lang], recv_sem=recv_sems.at[my_shard, lang],
-            device_id=(my_lang, to), device_id_type=MESH,
-        )
-
-    def from_shard(every, send_sems, recv_sems, lang, step):
-        origin = last_shard(step)
-        return pltpu.make_async_remote_copy(
-            src_ref=every.at[origin, lang], dst_ref=every.at[origin, lang],
-            send_sem=send_sems.at[origin, lang], recv_sem=recv_sems.at[origin, lang],
-            device_id=(my_lang, origin), device_id_type=MESH,
-        )
-
-    for step in range(1, shard_count):
-        over_shard(out_main.at[my_lang], *b_main, my_lang, step).start()
-    for d, k in steps:
-        over_lang(*a_main, d, k).start()
+    for d, k in steps:
         over_lang(*a_rest, d, k).start()
-    for step in range(1, shard_count):
+    for step in hops:
         over_shard(out_rest.at[my_lang], *b_rest, my_lang, step).start()
     all_main[my_shard, my_lang] = out_main[my_lang]
     all_rest[my_shard, my_lang] = out_rest[my_lang]
@@ -239,10 +269,10 @@
     def forward(d, k):
         lang = earlier(d, k)
         from_lang(*a_main, d, k).wait_recv()
-        for step in range(1, shard_count):
+        for step in hops:
             over_shard(all_main.at[my_shard, lang], *b_main, lang, step).start()
         from_lang(*a_rest, d, k).wait_recv()
-        for step in range(1, shard_count):
+        for step in hops:
             over_shard(all_rest.at[my_shard, lang], *b_rest, lang, step).start()
 
     def forward_group(d):
@@ -258,9 +288,11 @@
     ).T
     ret_rest[...] = jnp.zeros_like(ret_rest)
 
-    ahead = min(2, groups - 1)
+    ahead = min(3 if square else 2, groups - 1)
     for d in range(1, ahead + 1):
         forward_group(d)
+        if square and d <= 2:
+            relay_group(d - 1)
     load.wait()
     sign = (1 - 2 * lax.rem(my_shard, 2)).astype(jnp.float32)
 
@@ -284,12 +316,16 @@
         t[pl.ds(i, 1), :] = v[i % SUB:i % SUB + 1, :]
 
     def score(c, carry):
+        if square:
+            @pl.when(c + 2 < groups)
+            def _():
+                relay_group(c + 2)
+
         @pl.when(c < groups)
         def _():
             base = lax.rem(my_group + groups - c, groups) * group
             for k in range(group):
-                for step in range(1, shard_count):
-                    from_shard(*b_main, base + k, step).wait_recv()
+                await_others(b_main, base + k)
             for s in range(shard_count):
                 block[s * part:(s + 1) * part, :] = all_main[s, pl.ds(base, group)].reshape(
                     part, features
@@ -298,8 +334,7 @@
         @pl.when(c == groups)
         def _():
             for lang in range(langs):
-                for step in range(1, shard_count):
-                    from_shard(*b_rest, lang, step).wait_recv()
+                await_others(b_rest, lang)
 
         @pl.when(c >= groups)
         def _():
@@ -365,9 +400,12 @@
     back_rest[my_lang] = ret_rest[my_lang]
 
     def drain(lang, carry):
-        for step in range(1, shard_count):
+        for step in hops:
             over_shard(all_main.at[my_shard, lang], *b_main, lang, step).wait_send()
             over_shard(all_rest.at[my_shard, lang], *b_rest, lang, step).wait_send()
+        if square:
+            relay(*b_main, lang).wait_send()
+            relay(*b_rest, lang).wait_send()
         return carry
 
     def drain_answers(c, carry):

time: 37.1 us -> 39.7 us (1.070)
  Pallas kernels: 35.5 us -> 38.1 us
    pallas_call x1, Pallas kernels: 35.5 us -> 38.1 us  [shards(): pl.pallas_call(functools.partial(kernel, langs, shard_count), out_shape=j...]
where the time goes in v4:
time: 39.7 us; the launch traced here: 39.5 us
  Pallas kernels  38.1 us (96%)
  local copies, waits for them, and re-layouts  1.47 us (4%)
    pallas_call x1, Pallas kernels, shards(): pl.pallas_call(functools.partial(kernel, langs, shard_count), out_shape=j...  38.1 us
    unnamed x1, local copies, waits for them, and re-layouts  1.47 us

profile of v4, /device:TPU:0, one launch (start us, length us, event | category | flops | bytes accessed | tf_op | source)
XLA Modules:
  0.0 39.5 jit_solution(13655152621859986420)
XLA Ops:
  0.0 38.1 %shard_map.37 = f32[128,128]{1,0:T(8,128)} custom-call(bf16[128,768]{1,0:T(8,128)(2,1)} %q_ref.1, s32[1,128]{1,0:T(1,128)} %bitcast.1, bf16[1024,768]{1,0:T(8,128)(2,1)} %c_hbm.1), custom_call_target="tpu_custom_call" | custom-call | tf_op jit(solution)/shard_map/pallas_call | solution.py:446
  38.1 1.5 %copy.5 = f32[128,128]{1,0:T(8,128)} copy(f32[128,128]{1,0:T(8,128)} %shard_map.37) | data formatting | bytes 131072

commit v5 on v3

--- a/solution.py
+++ b/solution.py
@@ -258,7 +258,7 @@
     ).T
     ret_rest[...] = jnp.zeros_like(ret_rest)
 
-    ahead = min(2, groups - 1)
+    ahead = min(3, groups - 1)
     for d in range(1, ahead + 1):
         forward_group(d)
     load.wait()

time: 37.1 us -> 36.9 us (level)
  no operation moved by 1% of the time
where the time goes in v5:
time: 36.9 us; the launch traced here: 36.7 us
  Pallas kernels  35.2 us (95%)
  local copies, waits for them, and re-layouts  1.47 us (4%)
    pallas_call x1, Pallas kernels, shards(): pl.pallas_call(functools.partial(kernel, langs, shard_count), out_shape=j...  35.2 us
    unnamed x1, local copies, waits for them, and re-layouts  1.47 us

profile of v5, /device:TPU:0, one launch (start us, length us, event | category | flops | bytes accessed | tf_op | source)
XLA Modules:
  0.0 36.7 jit_solution(12154061646095555675)
XLA Ops:
  0.0 35.2 %shard_map.37 = f32[128,128]{1,0:T(8,128)} custom-call(bf16[128,768]{1,0:T(8,128)(2,1)} %q_ref.1, s32[1,128]{1,0:T(1,128)} %bitcast.1, bf16[1024,768]{1,0:T(8,128)(2,1)} %c_hbm.1), custom_call_target="tpu_custom_call" | custom-call | tf_op jit(solution)/shard_map/pallas_call | solution.py:408
  35.2 1.5 %copy.5 = f32[128,128]{1,0:T(8,128)} copy(f32[128,128]{1,0:T(8,128)} %shard_map.37) | data formatting | bytes 131072
